TPU v7x, 256 devices: a whole 4x4x8 slice. The times are simulated.
256 devices in a mesh: qa: 32 (over z, x_lo, core), qb: 8 (over y, x_hi).
Axes of the slice: x: 4 (x_hi: 2, x_lo: 2; x = x_hi * 2 + x_lo), y: 4, z: 8, core: 2. Of those that a mesh axis runs over, the one named last changes fastest.
Arguments:
- wave_parts: float32 [2, 2048, 128, 128], P(None, ('qa', 'qb')), may hold values from -6 to 6
- level_table: float32 [2048, 128, 128], P(('qa', 'qb')), may hold values from -2 to 2
- phase_angles: float32 [2, 128], replicated, may hold values from 0.3 to 1.2
Outputs:
- final_parts: float32 [2, 2048, 128, 128], P(None, ('qa', 'qb'))
All inputs are finite; a program needn't handle non-finite values.
Results may differ from a plain program's by a relative error of at most 0.0003.
Values sent between devices are 32-bit elements; how exact they have to be, the bound alone decides.
A program may use at most 64 MiB of HBM per device.

v0:
```python
import jax
import jax.numpy as jnp
from jax import lax
from jax.sharding import PartitionSpec as P

LAYERS = 2


def count_bits(values, count):
    places = jnp.arange(count.bit_length() - 1, dtype=jnp.int32)
    return jnp.sum(values[..., None] >> places & 1, axis=-1)


def sign_table(count):
    rank = jnp.arange(count, dtype=jnp.int32)
    parity = count_bits(rank[:, None] & rank[None, :], count) % 2
    real_part = jnp.where(parity == 1, -1.0, 1.0).astype(jnp.float32) * count ** (-0.5)
    return real_part


def turn_dim(values, dim):
    real_part = sign_table(values.shape[dim])
    moved = jnp.tensordot(values, real_part, axes=([dim], [0]), precision=lax.Precision.HIGHEST)
    return jnp.moveaxis(moved, -1, dim)


def turn_phase(values, levels, angle):
    turn = angle * levels
    return jnp.stack(
        [
            values[0] * jnp.cos(turn) + values[1] * jnp.sin(turn),
            values[1] * jnp.cos(turn) - values[0] * jnp.sin(turn),
        ]
    )


def body(wave_parts, level_table, phase_angles):
    values = wave_parts
    for layer in range(LAYERS):
        values = turn_phase(values, level_table, phase_angles[layer])
        values = turn_dim(values, 3)
        values = turn_dim(values, 2)
        moved = lax.all_to_all(values, "qa", split_axis=2, concat_axis=1, tiled=True)
        moved = turn_dim(moved, 1)
        values = lax.all_to_all(moved, "qa", split_axis=1, concat_axis=2, tiled=True)
        moved = lax.all_to_all(values, "qb", split_axis=3, concat_axis=1, tiled=True)
        spread = moved.reshape(2, lax.axis_size("qb"), -1, moved.shape[2], moved.shape[3])
        moved = turn_dim(spread, 1).reshape(moved.shape)
        values = lax.all_to_all(moved, "qb", split_axis=1, concat_axis=3, tiled=True)
    return values


def solution(mesh):
    in_specs = (P(None, ("qa", "qb"), None, None), P(("qa", "qb"), None, None), P())
    out_specs = P(None, ("qa", "qb"), None, None)
    return jax.shard_map(body, mesh=mesh, in_specs=in_specs, out_specs=out_specs, check_vma=False)
```

profile of v0, /device:TPU:1, one launch (start us, length us, event | category | flops | bytes accessed | tf_op | source)
XLA Modules:
  0.0 243.0 jit_solution(2702907584651793497)
XLA Ops:
  0.0 0.8 slice_bitcast_fusion
  0.9 3.1 %fusion.17 = (f32[1,8,128,128]{3,2,1,0:T(8,128)S(1)}, f32[1,8,128,128]{3,2,1,0:T(8,128)S(1)}) fusion(f32[2,8,128,128]{3,2,1,0:T(8,128)} %param.3, f32[8,128,128]{2,1,0:T(8,128)} %param.4, f32[128]{0:T(128)S(1)} %get-tuple-element.12), kind=kLoop, calls=%fused_computation.28 | loop fusion | flops 917504 | bytes 2621952 | tf_op jit(solution)/shard_map/stack | solution.py:29
  4.0 1.1 fusion
  5.1 1.0 convolution_bitcast_fusion.5
  6.0 1.4 copy.100
  7.4 11.0 %all-to-all-start = ((f32[2,8,128,128]{3,1,0,2:T(8,128)}), f32[2,8,128,128]{3,1,0,2:T(8,128)S(1)}, u32[]{:S(2)}, u32[]{:S(2)}) async-start(f32[2,8,128,128]{3,1,0,2:T(8,128)} %copy.100), calls=%async_computation | async-start | bytes 2097152 | tf_op jit(solution)/shard_map/all_to_all | solution.py:43
  18.5 0.7 and_reduce_fusion
  19.2 27.4 %all-to-all-done = f32[2,8,128,128]{3,1,0,2:T(8,128)S(1)} async-done(((f32[2,8,128,128]{3,1,0,2:T(8,128)}), f32[2,8,128,128]{3,1,0,2:T(8,128)S(1)}, u32[]{:S(2)}, u32[]{:S(2)}) %all-to-all-start) | async-done | bytes 1048608 | tf_op jit(solution)/shard_map/all_to_all | solution.py:43
  46.5 1.8 convolution_bitcast_fusion.4
  48.4 0.5 copy.104
  48.9 32.2 %all_to_all.135 = f32[2,256,4,128]{3,2,0,1:T(4,128)S(1)} all-to-all(f32[2,256,4,128]{3,2,0,1:T(4,128)S(1)} %copy.104), channel_id=1, replica_groups=mesh['qa'=32,'qb'=8] {'qa'}, dimensions={1} | all-to-all | bytes 2097152 | tf_op jit(solution)/shard_map/all_to_all | solution.py:45
  81.1 0.2 copy.173
  81.3 0.1 copy.106
  81.4 1.5 copy.107
  82.9 6.4 %all-to-all-start.2 = ((f32[2,8,128,128]{2,1,0,3:T(8,128)}), f32[2,8,128,128]{2,1,0,3:T(8,128)S(1)}, u32[]{:S(2)}, u32[]{:S(2)}) async-start(f32[2,8,128,128]{2,1,0,3:T(8,128)} %copy.107), calls=%async_computation.2 | async-start | bytes 2097152 | tf_op jit(solution)/shard_map/all_to_all | solution.py:46
  89.3 16.0 %all-to-all-done.2 = f32[2,8,128,128]{2,1,0,3:T(8,128)S(1)} async-done(((f32[2,8,128,128]{2,1,0,3:T(8,128)}), f32[2,8,128,128]{2,1,0,3:T(8,128)S(1)}, u32[]{:S(2)}, u32[]{:S(2)}) %all-to-all-start.2) | async-done | bytes 1048608 | tf_op jit(solution)/shard_map/all_to_all | solution.py:46
  105.3 1.6 convolution_bitcast_fusion.3
  106.9 0.2 copy.111
  107.1 0.1 copy.112
  107.3 20.2 %all_to_all.136 = f32[2,64,128,16]{2,3,0,1:T(8,128)S(1)} all-to-all(f32[2,64,128,16]{2,3,0,1:T(8,128)S(1)} %copy.112), channel_id=1, replica_groups=mesh['qa'=32,'qb'=8] {'qb'}, dimensions={1} | all-to-all | bytes 2097152 | tf_op jit(solution)/shard_map/all_to_all | solution.py:49
  127.4 0.1 copy.113
  127.5 0.1 fusion.88
  127.7 0.2 copy.117
  127.9 0.0 copy-start
  128.0 0.2 copy.115
  128.2 0.8 copy-done
  128.9 2.0 add_bitcast_fusion
  131.0 1.1 fusion.4
  132.1 1.0 convolution_bitcast_fusion.2
  133.0 0.5 copy.121
  133.6 33.4 %all_to_all.137 = f32[2,8,128,128]{3,1,0,2:T(8,128)S(1)} all-to-all(f32[2,8,128,128]{3,1,0,2:T(8,128)S(1)} %copy.121), channel_id=1, replica_groups=mesh['qa'=32,'qb'=8] {'qa'}, dimensions={2} | all-to-all | bytes 2097152 | tf_op jit(solution)/shard_map/all_to_all | solution.py:43
  167.0 1.8 convolution_bitcast_fusion.1
  168.8 0.5 copy.125
  169.4 32.2 %all_to_all.138 = f32[2,256,4,128]{3,2,0,1:T(4,128)S(1)} all-to-all(f32[2,256,4,128]{3,2,0,1:T(4,128)S(1)} %copy.125), channel_id=1, replica_groups=mesh['qa'=32,'qb'=8] {'qa'}, dimensions={1} | all-to-all | bytes 2097152 | tf_op jit(solution)/shard_map/all_to_all | solution.py:45
  201.6 0.2 copy.172
  201.8 0.1 copy.127
  201.9 0.6 copy.128
  202.5 18.8 %all_to_all.139 = f32[2,8,128,128]{2,1,0,3:T(8,128)S(1)} all-to-all(f32[2,8,128,128]{2,1,0,3:T(8,128)S(1)} %copy.128), channel_id=1, replica_groups=mesh['qa'=32,'qb'=8] {'qb'}, dimensions={3} | all-to-all | bytes 2097152 | tf_op jit(solution)/shard_map/all_to_all | solution.py:46
  221.3 1.6 convolution_bitcast_fusion
  222.9 0.2 copy.132
  223.1 0.1 copy.133
  223.3 18.3 %all_to_all.140 = f32[2,64,128,16]{2,3,0,1:T(8,128)S(1)} all-to-all(f32[2,64,128,16]{2,3,0,1:T(8,128)S(1)} %copy.133), channel_id=1, replica_groups=mesh['qa'=32,'qb'=8] {'qb'}, dimensions={1} | all-to-all | bytes 2097152 | tf_op jit(solution)/shard_map/all_to_all | solution.py:49
  241.6 0.1 copy.135
  241.7 1.3 copy.136
  (8 shorter events, 0.2 us)
Async XLA Ops:
  7.4 39.1 %all-to-all-start = ((f32[2,8,128,128]{3,1,0,2:T(8,128)}), f32[2,8,128,128]{3,1,0,2:T(8,128)S(1)}, u32[]{:S(2)}, u32[]{:S(2)}) async-start(f32[2,8,128,128]{3,1,0,2:T(8,128)} %copy.100), calls=%async_computation | async-start | bytes 2097152 | tf_op jit(solution)/shard_map/all_to_all | solution.py:43
  82.9 22.3 %all-to-all-start.2 = ((f32[2,8,128,128]{2,1,0,3:T(8,128)}), f32[2,8,128,128]{2,1,0,3:T(8,128)S(1)}, u32[]{:S(2)}, u32[]{:S(2)}) async-start(f32[2,8,128,128]{2,1,0,3:T(8,128)} %copy.107), calls=%async_computation.2 | async-start | bytes 2097152 | tf_op jit(solution)/shard_map/all_to_all | solution.py:46
  127.9 1.0 copy-start
where the time goes:
time: 245 us; the launch traced here: 243 us
  blocking collectives  155 us (63%)
  waiting for transfers between devices  43.3 us (18%)
  starting transfers between devices  17.4 us (7%)
  matrix products  11.1 us (5%)
  local copies, waits for them, and re-layouts  9.96 us (4%)
  other arithmetic  5.88 us (2%)
    all_to_all x2, blocking collectives, body(): lax.all_to_all(moved, 'qa', split_axis=1, concat_axis=2, tiled=True)  64.4 us
    all_to_all x2, blocking collectives, body(): lax.all_to_all(moved, 'qb', split_axis=1, concat_axis=3, tiled=True)  38.5 us
    all_to_all x1, blocking collectives, body(): lax.all_to_all(values, 'qa', split_axis=2, concat_axis=1, tiled=True)  33.4 us
    all_to_all x1, waiting for transfers between devices, body(): lax.all_to_all(values, 'qa', split_axis=2, concat_axis=1, tiled=True)  27.4 us
    all_to_all x1, blocking collectives, body(): lax.all_to_all(values, 'qb', split_axis=3, concat_axis=1, tiled=True)  18.8 us
    all_to_all x1, waiting for transfers between devices, body(): lax.all_to_all(values, 'qb', split_axis=3, concat_axis=1, tiled=True)  16 us
    dot_general x8, matrix products, turn_dim(): jnp.tensordot(values, real_part, axes=([dim], [0]), precision=lax.Precisi...  11.1 us
    all_to_all x1, starting transfers between devices, body(): lax.all_to_all(values, 'qa', split_axis=2, concat_axis=1, tiled=True)  11 us
  transfers between devices with their start and end apart: 2, of which 2 were waited for; matrix products, arithmetic and copies ran while one was open for 0% of the time, Pallas kernels for 0%

commit v1 on v0

v1 whole, which is shorter than its diff:
```python
import functools

import jax
import jax.numpy as jnp
from jax import lax
from jax.experimental import pallas as pl
from jax.experimental.pallas import tpu as pltpu
from jax.sharding import PartitionSpec as P

MESH = pl.DeviceIdType.MESH
SCALE = 2.0**-12.5
CHIPS = 128


def place():
    qa, qb = lax.axis_index("qa"), lax.axis_index("qb")
    return qa // 4, (qa // 2) % 2 * 8 + qb, qa % 2


def device(z, w, core):
    return (z * 4 + w // 8 * 2 + core, w % 8)


def plane_step(w, d):
    xlo = (w // 8 + d // 8) % 2
    y = (w // 2 % 4 + d // 2 % 4) % 4
    xhi = (w % 2 + d % 2) % 2
    return xlo * 8 + y * 2 + xhi


def fwht(tiles):
    tiles = list(tiles)
    step = 1
    while step < len(tiles):
        for i in range(len(tiles)):
            if not i & step:
                u, v = tiles[i], tiles[i + step]
                tiles[i], tiles[i + step] = u + v, u - v
        step *= 2
    return tiles


def sign_matrix(count):
    both = lax.broadcasted_iota(jnp.int32, (count, count), 0) & lax.broadcasted_iota(jnp.int32, (count, count), 1)
    for shift in (4, 2, 1):
        both = both ^ (both >> shift)
    return (1 - 2 * (both & 1)).astype(jnp.float32).astype(jnp.bfloat16)


def halves(x):
    high = x.astype(jnp.bfloat16)
    return high, (x - high.astype(jnp.float32)).astype(jnp.bfloat16)


def turn_lanes(x, signs):
    high, low = halves(x)
    dot = functools.partial(jnp.dot, preferred_element_type=jnp.float32)
    return dot(high, signs) + dot(low, signs)


def turn_rows(x, signs):
    high, low = halves(x)
    dot = functools.partial(jnp.dot, preferred_element_type=jnp.float32)
    return dot(signs, high) + dot(signs, low)


def kernel(
    wave_ref, level_ref, angle_ref, out_ref,
    wave, level, local, local_in, send, recv, level_in, cos2, sin2, mix, mix_in, back, back_in, final,
    in_sem, out_sem, pair_send, pair_recv, level_send, level_recv, there_send, there_recv, back_send, back_recv, ready,
):
    z, w, core = place()
    me = z * 16 + w
    partner = device(z, w, 1 - core)
    own_sign = (1 - 2 * core).astype(jnp.float32)

    barrier = pltpu.get_barrier_semaphore()

    def signal(sem, to):
        pl.semaphore_signal(sem, inc=1, device_id=to, device_id_type=MESH)

    @pl.loop(1, 8)
    def _(d):
        signal(barrier, device((z + d) % 8, w, core))

    @pl.loop(1, 16)
    def _(d):
        signal(barrier, device(z, plane_step(w, d), core))

    signal(barrier, partner)

    level_copy = pltpu.make_async_copy(level_ref, level, in_sem.at[0])
    wave_copy = pltpu.make_async_copy(wave_ref, wave, in_sem.at[1])
    level_copy.start()
    wave_copy.start()
    signs = sign_matrix(128)
    level_copy.wait()

    pl.semaphore_wait(barrier, 23)

    @pl.loop(1, 16)
    def _(d):
        signal(ready, device(z, plane_step(w, d), core))

    pl.semaphore_wait(ready, 15)

    def peer(m):
        d = m % 8 * 16 + m // 8
        return (z + d // 16) % 8, plane_step(w, d % 16)

    @pl.loop(1, CHIPS)
    def _(m):
        pz, pw = peer(m)
        pltpu.make_async_remote_copy(
            level.at[pz, pl.ds(pw * 8, 8)], level_in.at[me], level_send, level_recv,
            device_id=device(pz, pw, core), device_id_type=MESH,
        ).start()

    wave_copy.wait()

    @pl.loop(0, 8)
    def _(b):
        turn = angle_ref[0:1] * level[b]
        c, s = jnp.cos(turn) * SCALE, jnp.sin(turn) * SCALE
        re, im = wave[0, b], wave[1, b]
        for part, x in enumerate((re * c + im * s, im * c - re * s)):
            local[part, b] = turn_rows(turn_lanes(x, signs), signs)

    @pl.loop(0, 16)
    def _(t):
        rows = pl.ds(t * 8, 8)
        for part in range(2):
            for b, x in enumerate(fwht([local[part, b, rows] for b in range(8)])):
                local[part, b, rows] = x

    swap = pltpu.make_async_remote_copy(
        local, local_in, pair_send.at[0], pair_recv.at[0], device_id=partner, device_id_type=MESH
    )
    swap.start()
    swap.wait()

    lower = lax.broadcasted_iota(jnp.int32, (8, 128), 0) < 4

    @pl.loop(0, 8)
    def _(b):
        for t in range(16):
            rows = pl.ds(t * 8, 8)
            re, im = (local_in[part, b, rows] + own_sign * local[part, b, rows] for part in range(2))
            send[0, b * 16 + t] = jnp.where(lower, re, pltpu.roll(im, 4, 0))
            send[1, b * 16 + t] = jnp.where(lower, pltpu.roll(re, 4, 0), im)

    def spread(src, dst, send_sem, recv_sem):
        @pl.loop(1, CHIPS)
        def _(m):
            pz, pw = peer(m)
            pltpu.make_async_remote_copy(
                src.at[pz * 16 + pw], dst.at[me], send_sem, recv_sem,
                device_id=device(pz, pw, core), device_id_type=MESH,
            ).start()

    def gathered(src, dst, send_sem, recv_sem):
        return pltpu.make_async_remote_copy(
            src.at[pl.ds(0, CHIPS - 1)], dst.at[pl.ds(0, CHIPS - 1)], send_sem, recv_sem,
            device_id=partner, device_id_type=MESH,
        )

    for k in range(2):
        spread(send.at[k], recv.at[k], there_send.at[k], there_recv.at[k])
        recv[k, me] = send[k, me]
    level_in[me] = level[z, pl.ds(w * 8, 8)]

    gathered(level_in, level_in, level_send, level_recv).wait_recv()

    @pl.loop(0, CHIPS)
    def _(t):
        turn = angle_ref[1:2] * level_in[t]
        cos2[t] = jnp.cos(turn) * SCALE
        sin2[t] = jnp.sin(turn) * SCALE

    sublane = lax.broadcasted_iota(jnp.int32, (8, 128), 0)

    def turn_sublanes(x, step):
        upper = (sublane & step) != 0
        other = jnp.where(upper, pltpu.roll(x, step, 0), pltpu.roll(x, 8 - step, 0))
        return other + jnp.where(upper, -x, x)

    for k in range(2):
        gathered(send.at[k], recv.at[k], there_send.at[k], there_recv.at[k]).wait_recv()

        @pl.loop(0, 8)
        def _(i):
            for j, x in enumerate(fwht([recv[k, i * 16 + j] for j in range(16)])):
                recv[k, i * 16 + j] = x

        @pl.loop(0, 16)
        def _(j):
            tiles = fwht([recv[k, i * 16 + j] for i in range(8)])
            for i in range(8):
                c, s = cos2[i * 16 + j], sin2[i * 16 + j]
                if k == 0:
                    c, s = jnp.where(lower, c, pltpu.roll(c, 4, 0)), jnp.where(lower, s, -pltpu.roll(s, 4, 0))
                else:
                    c, s = jnp.where(lower, pltpu.roll(c, 4, 0), c), jnp.where(lower, pltpu.roll(s, 4, 0), -s)
                tiles[i] = tiles[i] * c + pltpu.roll(tiles[i], 4, 0) * s
            for i, x in enumerate(fwht(tiles)):
                recv[k, i * 16 + j] = x

        @pl.loop(0, 8)
        def _(i):
            tiles = fwht([recv[k, i * 16 + j] for j in range(16)])
            tiles = [turn_sublanes(turn_sublanes(x, 1), 2) for x in tiles]
            x = turn_lanes(jnp.concatenate(tiles, axis=0), signs)
            for j in range(16):
                mix[k, i * 16 + j] = x[j * 8 : j * 8 + 8]

        swap = pltpu.make_async_remote_copy(
            mix.at[k], mix_in.at[k], pair_send.at[1 + k], pair_recv.at[1 + k], device_id=partner, device_id_type=MESH
        )
        swap.start()
        swap.wait()

        @pl.loop(0, 8)
        def _(i):
            for j in range(16):
                t = i * 16 + j
                back[k, t] = mix_in[k, t] + own_sign * mix[k, t]

        spread(back.at[k], back_in.at[k], back_send.at[k], back_recv.at[k])
        back_in[k, me] = back[k, me]

    for k in range(2):
        gathered(back.at[k], back_in.at[k], back_send.at[k], back_recv.at[k]).wait_recv()

        @pl.loop(0, 8)
        def _(i):
            for j, x in enumerate(fwht([back_in[k, i * 16 + j] for j in range(16)])):
                back_in[k, i * 16 + j] = x

    @pl.loop(0, 16)
    def _(j):
        first, second = (fwht([back_in[k, i * 16 + j] for i in range(8)]) for k in range(2))
        rows = pl.ds(j * 8, 8)
        for i in range(8):
            u, v = first[i] + second[i], first[i] - second[i]
            final[0, i, rows] = jnp.where(lower, u, pltpu.roll(v, 4, 0))
            final[1, i, rows] = jnp.where(lower, pltpu.roll(u, 4, 0), v)

    out_copy = pltpu.make_async_copy(final, out_ref, out_sem)
    out_copy.start()
    gathered(level_in, level_in, level_send, level_recv).wait_send()
    for k in range(2):
        gathered(send.at[k], recv.at[k], there_send.at[k], there_recv.at[k]).wait_send()
        gathered(back.at[k], back_in.at[k], back_send.at[k], back_recv.at[k]).wait_send()
    out_copy.wait()


def body(wave_parts, level_table, phase_angles):
    f32 = jnp.float32
    state, tiles = pltpu.VMEM((2, 8, 128, 128), f32), pltpu.VMEM((2, CHIPS, 8, 128), f32)
    table = pltpu.VMEM((CHIPS, 8, 128), f32)
    dma = pltpu.SemaphoreType.DMA
    anywhere = pl.BlockSpec(memory_space=pl.ANY)
    return pl.pallas_call(
        kernel,
        out_shape=jax.ShapeDtypeStruct(wave_parts.shape, f32),
        in_specs=[anywhere, anywhere, pl.BlockSpec(memory_space=pltpu.VMEM)],
        out_specs=anywhere,
        scratch_shapes=[
            state, pltpu.VMEM((8, 128, 128), f32), state, state, tiles, tiles, table, table, table, tiles, tiles, tiles, tiles, state,
            dma((2,)), dma, dma((3,)), dma((3,)), dma, dma, dma((2,)), dma((2,)), dma((2,)), dma((2,)), pltpu.SemaphoreType.REGULAR,
        ],
        compiler_params=pltpu.CompilerParams(collective_id=0, has_side_effects=True),
    )(wave_parts, level_table, phase_angles)


def solution(mesh):
    in_specs = (P(None, ("qa", "qb"), None, None), P(("qa", "qb"), None, None), P())
    out_specs = P(None, ("qa", "qb"), None, None)
    return jax.shard_map(body, mesh=mesh, in_specs=in_specs, out_specs=out_specs, check_vma=False)
```

time: 245 us -> 81.8 us (0.33)
  blocking collectives: 155 us -> 0 us
  Pallas kernels: 0 us -> 79.4 us
  waiting for transfers between devices: 43.3 us -> 0 us
  starting transfers between devices: 17.4 us -> 0 us
  matrix products: 11.1 us -> 0 us
  local copies, waits for them, and re-layouts: 9.96 us -> 2.3 us
  other arithmetic: 5.88 us -> 0 us
    all_to_all x6 -> x0, blocking collectives: 155 us -> none  [the longest x2 64.4 us: body(): lax.all_to_all(moved, 'qa', split_axis=1, concat_axis=2, tiled=True)]
    pallas_call x0 -> x1, Pallas kernels: none -> 79.4 us  [body(): pl.pallas_call(kernel, out_shape=jax.ShapeDtypeStruct(wave_parts.shape, f...]
    all_to_all x2 -> x0, waiting for transfers between devices: 43.3 us -> none  [the longest x1 27.4 us: body(): lax.all_to_all(values, 'qa', split_axis=2, concat_axis=1, tiled=True)]
    all_to_all x2 -> x0, starting transfers between devices: 17.4 us -> none  [the longest x1 11 us: body(): lax.all_to_all(values, 'qa', split_axis=2, concat_axis=1, tiled=True)]
    dot_general x8 -> x0, matrix products: 11.1 us -> none  [turn_dim(): jnp.tensordot(values, real_part, axes=([dim], [0]), precision=lax.Precisi...]
    another operation x2 -> x0, other arithmetic: 5.09 us -> none  [turn_phase(): jnp.stack([values[0] * jnp.cos(turn) + values[1] * jnp.sin(turn), values[...]
    all_to_all x9 -> x0, local copies, waits for them, and re-layouts: 4.24 us -> none  [the longest x6 2.75 us: body(): lax.all_to_all(moved, 'qa', split_axis=1, concat_axis=2, tiled=True)]
    transpose x6 -> x0, local copies, waits for them, and re-layouts: 3.33 us -> none  [turn_dim(): return jnp.moveaxis(moved, -1, dim)]
  transfers between devices with their start and end apart: 2 -> 0, of which waited for: 2 -> 0; matrix products, arithmetic and copies ran while one was open for 0% -> 0% of each run, Pallas kernels for 0% -> 0%
where the time goes in v1:
time: 81.8 us; the launch traced here: 81.7 us
  Pallas kernels  79.4 us (97%)
  local copies, waits for them, and re-layouts  2.3 us (3%)
    pallas_call x1, Pallas kernels, body(): pl.pallas_call(kernel, out_shape=jax.ShapeDtypeStruct(wave_parts.shape, f...  79.4 us
    unnamed x1, local copies, waits for them, and re-layouts  2.3 us

profile of v1, /device:TPU:1, one launch (start us, length us, event | category | flops | bytes accessed | tf_op | source)
XLA Modules:
  0.0 81.7 jit_solution(13548532721710925035)
XLA Ops:
  0.0 79.4 %shard_map.37 = f32[2,8,128,128]{3,2,1,0:T(8,128)} custom-call(f32[2,8,128,128]{3,2,1,0:T(8,128)} %wave_ref.1, f32[8,128,128]{2,1,0:T(8,128)} %level_ref.1, f32[2,128]{1,0:T(2,128)} %angle_ref.1), custom_call_target="tpu_custom_call" | custom-call | tf_op jit(solution)/shard_map/pallas_call | solution.py:263
  79.4 2.3 %copy.5 = f32[2,8,128,128]{3,2,1,0:T(8,128)} copy(f32[2,8,128,128]{3,2,1,0:T(8,128)} %shard_map.37) | data formatting | bytes 2097152

commit v2 on v1

v2 whole, which is shorter than its diff:
```python
import functools

import jax
import jax.numpy as jnp
from jax import lax
from jax.experimental import pallas as pl
from jax.experimental.pallas import tpu as pltpu
from jax.sharding import PartitionSpec as P

MESH = pl.DeviceIdType.MESH
SCALE = 2.0**-12.5
CHIPS = 128


def place():
    qa, qb = lax.axis_index("qa"), lax.axis_index("qb")
    return qa // 4, (qa // 2) % 2 * 8 + qb, qa % 2


def device(z, w, core):
    return (z * 4 + w // 8 * 2 + core, w % 8)


def plane_step(w, d):
    xlo = (w // 8 + d // 8) % 2
    y = (w // 2 % 4 + d // 2 % 4) % 4
    xhi = (w % 2 + d % 2) % 2
    return xlo * 8 + y * 2 + xhi


def fwht(tiles):
    tiles = list(tiles)
    step = 1
    while step < len(tiles):
        for i in range(len(tiles)):
            if not i & step:
                u, v = tiles[i], tiles[i + step]
                tiles[i], tiles[i + step] = u + v, u - v
        step *= 2
    return tiles


def sign_matrix(count):
    both = lax.broadcasted_iota(jnp.int32, (count, count), 0) & lax.broadcasted_iota(jnp.int32, (count, count), 1)
    for shift in (4, 2, 1):
        both = both ^ (both >> shift)
    return (1 - 2 * (both & 1)).astype(jnp.float32).astype(jnp.bfloat16)


def halves(x):
    high = x.astype(jnp.bfloat16)
    return high, (x - high.astype(jnp.float32)).astype(jnp.bfloat16)


def turn_lanes(x, signs):
    high, low = halves(x)
    dot = functools.partial(jnp.dot, preferred_element_type=jnp.float32)
    return dot(high, signs) + dot(low, signs)


def turn_rows(x, signs):
    high, low = halves(x)
    dot = functools.partial(jnp.dot, preferred_element_type=jnp.float32)
    return dot(signs, high) + dot(signs, low)


def kernel(
    wave_ref, level_ref, angle_hbm, out_ref,
    wave, level, angle_ref, cosine, sine, local, local_in, send, recv, level_mid, level_in, mix, mix_in, back, back_in,
    in_sem, pair_send, pair_recv, mid_send, mid_recv, level_send, level_recv, there_send, there_recv, back_send, back_recv, ready,
):
    z, w, core = place()
    me = z * 16 + w
    partner = device(z, w, 1 - core)
    own_sign = (1 - 2 * core).astype(jnp.float32)
    lower = lax.broadcasted_iota(jnp.int32, (8, 128), 0) < 4

    barrier = pltpu.get_barrier_semaphore()

    def signal(sem, to):
        pl.semaphore_signal(sem, inc=1, device_id=to, device_id_type=MESH)

    def send_to(src, dst, send_sem, recv_sem, to):
        return pltpu.make_async_remote_copy(src, dst, send_sem, recv_sem, device_id=to, device_id_type=MESH)

    level_copy = pltpu.make_async_copy(level_ref, level, in_sem.at[0])
    wave_copy = pltpu.make_async_copy(wave_ref, wave, in_sem.at[1])
    level_copy.start()
    angle_copy = pltpu.make_async_copy(angle_hbm, angle_ref, in_sem.at[2])
    angle_copy.start()
    wave_copy.start()

    @pl.loop(1, 8)
    def _(d):
        signal(barrier, device((z + d) % 8, w, core))

    @pl.loop(1, 16)
    def _(d):
        signal(barrier, device(z, plane_step(w, d), core))

    signal(barrier, partner)

    signs = sign_matrix(128)
    level_copy.wait()

    pl.semaphore_wait(barrier, 23)
    for d in (4, 3, 5, 2, 6, 1, 7):
        there = (z + d) % 8
        send_to(level.at[there], level_mid.at[z], mid_send, mid_recv.at[d - 1], device(there, w, core)).start()

    @pl.loop(1, 16)
    def _(d):
        signal(ready, device(z, plane_step(w, d), core))

    angle_copy.wait()
    wave_copy.wait()

    @pl.loop(0, 8)
    def _(b):
        turn = angle_ref[0:1] * level[b]
        c, s = jnp.cos(turn) * SCALE, jnp.sin(turn) * SCALE
        re, im = wave[0, b], wave[1, b]
        for part, x in enumerate((re * c + im * s, im * c - re * s)):
            local[part, b] = turn_rows(turn_lanes(x, signs), signs)

    level_mid[z] = level[z]

    def swap(q):
        rows = pl.ds(q * 32, 32)
        return send_to(
            local.at[:, :, rows], local_in.at[:, :, rows], pair_send.at[q], pair_recv.at[q], partner
        )

    for q in range(4):

        @pl.loop(q * 4, q * 4 + 4)
        def _(t):
            rows = pl.ds(t * 8, 8)
            for part in range(2):
                for b, x in enumerate(fwht([local[part, b, rows] for b in range(8)])):
                    local[part, b, rows] = x

        swap(q).start()

    for q in range(4):
        swap(q).wait_recv()

        @pl.loop(0, 8)
        def _(b):
            for t in range(q * 4, q * 4 + 4):
                rows = pl.ds(t * 8, 8)
                re, im = (local_in[part, b, rows] + own_sign * local[part, b, rows] for part in range(2))
                send[0, b * 16 + t] = jnp.where(lower, re, pltpu.roll(im, 4, 0))
                send[1, b * 16 + t] = jnp.where(lower, pltpu.roll(re, 4, 0), im)

    def spread(src, dst, send_sem, recv_sem):
        for d in (4, 3, 5, 2, 6, 1, 7, 0):

            @pl.loop(0 if d else 1, 16)
            def _(e):
                pz, pw = (z + d) % 8, plane_step(w, e)
                send_to(src.at[pz * 16 + pw], dst.at[me], send_sem, recv_sem, device(pz, pw, core)).start()

    def gathered(src, dst, send_sem, recv_sem):
        return send_to(src.at[pl.ds(0, CHIPS - 1)], dst.at[pl.ds(0, CHIPS - 1)], send_sem, recv_sem, partner)

    def there(k):
        return send.at[k], recv.at[k], there_send.at[k], there_recv.at[k]

    def again(k):
        return back.at[k], back_in.at[k], back_send.at[k], back_recv.at[k]

    pl.semaphore_wait(ready, 15)
    spread(*there(0))
    recv[0, me] = send[0, me]

    for d in (1, 7, 2, 6, 3, 5, 4):
        source = (z + d) % 8
        send_to(
            level.at[0], level_mid.at[source], mid_send, mid_recv.at[7 - d], device(source, w, core)
        ).wait_recv()

    @pl.loop(1, 16)
    def _(e):
        pw = plane_step(w, e)
        send_to(
            level_mid.at[:, pl.ds(pw * 8, 8)], level_in.at[:, w], level_send, level_recv, device(z, pw, core)
        ).start()

    level_in[:, w] = level_mid[:, pl.ds(w * 8, 8)]
    spread(*there(1))
    recv[1, me] = send[1, me]
    level_part = level_in.at[:, pl.ds(0, 15)]
    level_all = send_to(level_part, level_part, level_send, level_recv, partner)
    level_all.wait_recv()

    @pl.loop(0, 8)
    def _(i):
        turn = angle_ref[1:2] * level_in[i].reshape(128, 128)
        cosine[i] = (jnp.cos(turn) * SCALE).reshape(16, 8, 128)
        sine[i] = (jnp.sin(turn) * SCALE).reshape(16, 8, 128)

    sublane = lax.broadcasted_iota(jnp.int32, (8, 128), 0)

    def turn_sublanes(x, step):
        upper = (sublane & step) != 0
        other = jnp.where(upper, pltpu.roll(x, step, 0), pltpu.roll(x, 8 - step, 0))
        return other + jnp.where(upper, -x, x)

    for k in range(2):
        gathered(*there(k)).wait_recv()

        @pl.loop(0, 8)
        def _(i):
            for j, x in enumerate(fwht([recv[k, i * 16 + j] for j in range(16)])):
                recv[k, i * 16 + j] = x

        @pl.loop(0, 16)
        def _(j):
            tiles = fwht([recv[k, i * 16 + j] for i in range(8)])
            for i in range(8):
                c, s = cosine[i, j], sine[i, j]
                if k == 0:
                    c, s = jnp.where(lower, c, pltpu.roll(c, 4, 0)), jnp.where(lower, s, -pltpu.roll(s, 4, 0))
                else:
                    c, s = jnp.where(lower, pltpu.roll(c, 4, 0), c), jnp.where(lower, pltpu.roll(s, 4, 0), -s)
                tiles[i] = tiles[i] * c + pltpu.roll(tiles[i], 4, 0) * s
            for i, x in enumerate(fwht(tiles)):
                recv[k, i * 16 + j] = x

        @pl.loop(0, 8)
        def _(i):
            tiles = fwht([recv[k, i * 16 + j] for j in range(16)])
            tiles = [turn_sublanes(turn_sublanes(x, 1), 2) for x in tiles]
            x = turn_lanes(jnp.concatenate(tiles, axis=0), signs)
            for j in range(16):
                mix[k, i * 16 + j] = x[j * 8 : j * 8 + 8]

        pair = send_to(mix.at[k], mix_in.at[k], pair_send.at[4 + k], pair_recv.at[4 + k], partner)
        pair.start()
        pair.wait()

        @pl.loop(0, 8)
        def _(i):
            for j in range(16):
                t = i * 16 + j
                back[k, t] = mix_in[k, t] + own_sign * mix[k, t]

        spread(*again(k))
        back_in[k, me] = back[k, me]

    for q in range(4):
        swap(q).wait_send()
    for d in range(7):
        send_to(level.at[0], level_mid.at[0], mid_send, mid_recv.at[0], partner).wait_send()
    level_all.wait_send()
    for k in range(2):
        gathered(*there(k)).wait_send()

    for k in range(2):
        gathered(*again(k)).wait_recv()

        @pl.loop(0, 8)
        def _(i):
            for j, x in enumerate(fwht([back_in[k, i * 16 + j] for j in range(16)])):
                out_ref[k, i * 16 + j] = x

    for k in range(2):
        gathered(*again(k)).wait_send()


def finish(tiles_ref, out_ref, final, out_sem):
    lower = lax.broadcasted_iota(jnp.int32, (8, 128), 0) < 4
    copies = []
    for q in range(4):

        @pl.loop(q * 4, q * 4 + 4)
        def _(j):
            first, second = (fwht([tiles_ref[k, i * 16 + j] for i in range(8)]) for k in range(2))
            rows = pl.ds(j * 8, 8)
            for i in range(8):
                u, v = first[i] + second[i], first[i] - second[i]
                final[0, i, rows] = jnp.where(lower, u, pltpu.roll(v, 4, 0))
                final[1, i, rows] = jnp.where(lower, pltpu.roll(u, 4, 0), v)

        rows = pl.ds(q * 32, 32)
        copies.append(pltpu.make_async_copy(final.at[:, :, rows], out_ref.at[:, :, rows], out_sem.at[q]))
        copies[-1].start()
    for copy in copies:
        copy.wait()


def body(wave_parts, level_table, phase_angles):
    f32 = jnp.float32
    state, tiles = pltpu.VMEM((2, 8, 128, 128), f32), pltpu.VMEM((2, CHIPS, 8, 128), f32)
    table = pltpu.VMEM((8, 16, 8, 128), f32)
    blocks = pltpu.VMEM((8, 128, 128), f32)
    dma = pltpu.SemaphoreType.DMA
    anywhere, on_chip = pl.BlockSpec(memory_space=pl.ANY), pl.BlockSpec(memory_space=pltpu.VMEM)
    off_chip = pl.BlockSpec(memory_space=pltpu.HBM)
    args = [pltpu.with_memory_space_constraint(x, pltpu.HBM) for x in (wave_parts, level_table, phase_angles)]
    mixed = pl.pallas_call(
        kernel,
        out_shape=pltpu.VMEM((2, CHIPS, 8, 128), f32),
        in_specs=[off_chip] * 3,
        out_specs=on_chip,
        scratch_shapes=[
            state, blocks, pltpu.VMEM((2, 128), f32), table, table, state, state, tiles, tiles, blocks, table, tiles, tiles, tiles, tiles,
            dma((3,)), dma((6,)), dma((6,)), dma, dma((7,)), dma, dma, dma((2,)), dma((2,)), dma((2,)), dma((2,)), pltpu.SemaphoreType.REGULAR,
        ],
        compiler_params=pltpu.CompilerParams(collective_id=0, has_side_effects=True, vmem_limit_bytes=32 * 2**20),
    )(*args)
    return pl.pallas_call(
        finish,
        out_shape=jax.ShapeDtypeStruct(wave_parts.shape, f32),
        in_specs=[on_chip],
        out_specs=anywhere,
        scratch_shapes=[state, dma((4,))],
        compiler_params=pltpu.CompilerParams(vmem_limit_bytes=16 * 2**20),
    )(mixed)


def solution(mesh):
    in_specs = (P(None, ("qa", "qb"), None, None), P(("qa", "qb"), None, None), P())
    out_specs = P(None, ("qa", "qb"), None, None)
    return jax.shard_map(body, mesh=mesh, in_specs=in_specs, out_specs=out_specs, check_vma=False)
```

time: 81.8 us -> 73.7 us (0.901)
  Pallas kernels: 79.4 us -> 73.6 us
  local copies, waits for them, and re-layouts: 2.3 us -> 0 us
    pallas_call x1 -> x2, Pallas kernels: 79.4 us -> 73.6 us  [the longest x1 72.6 us: body(): pl.pallas_call(kernel, out_shape=pltpu.VMEM((2, CHIPS, 8, 128), f32), in_...]
    unnamed x1 -> x0, local copies, waits for them, and re-layouts: 2.3 us -> none
where the time goes in v2:
time: 73.7 us
  Pallas kernels  73.6 us (100%)
    pallas_call x1, Pallas kernels, body(): pl.pallas_call(kernel, out_shape=pltpu.VMEM((2, CHIPS, 8, 128), f32), in_...  72.6 us

profile of v2, /device:TPU:1, one launch (start us, length us, event | category | flops | bytes accessed | tf_op | source)
XLA Modules:
  0.0 73.7 jit_solution(12606369724762592807)
XLA Ops:
  0.0 72.6 %shard_map.37.tiles_ref = f32[2,128,8,128]{3,2,1,0:T(8,128)S(1)} custom-call(f32[2,8,128,128]{3,2,1,0:T(8,128)} %wave_ref.1, f32[8,128,128]{2,1,0:T(8,128)} %level_ref.1, f32[2,128]{1,0:T(2,128)} %angle_hbm.1), custom_call_target="tpu_custom_call" | custom-call | tf_op jit(solution)/shard_map/pallas_call | solution.py:302
  72.6 1.1 %shard_map.38 = f32[2,8,128,128]{3,2,1,0:T(8,128)} custom-call(f32[2,128,8,128]{3,2,1,0:T(8,128)S(1)} %shard_map.37.tiles_ref), custom_call_target="tpu_custom_call" | custom-call | tf_op jit(solution)/shard_map/pallas_call | solution.py:313

commit v3 on v2

--- a/solution.py
+++ b/solution.py
@@ -10,6 +10,9 @@
 MESH = pl.DeviceIdType.MESH
 SCALE = 2.0**-12.5
 CHIPS = 128
+FAR_FIRST = (5, 3, 7, 12, 13, 1, 4, 10, 11, 14, 15, 2, 6, 8, 9, 0)
+COS = (0.9999999995270198, -0.49999999256864547, 0.04166664759094903, -0.0013888705067878636, 2.479313621797957e-05, -2.7357116288633015e-07, 1.850280961043466e-09)
+SIN = (0.9999999957579141, -0.1666666176642379, 0.008333241511668515, -0.00019834965410918986, 2.7360914118386437e-06, -2.2205074368871847e-08)
 
 
 def place():
@@ -19,6 +22,10 @@
 
 def device(z, w, core):
     return (z * 4 + w // 8 * 2 + core, w % 8)
+
+
+def plane(x, y):
+    return x % 2 * 8 + y * 2 + x // 2
 
 
 def plane_step(w, d):
@@ -40,6 +47,18 @@
     return tiles
 
 
+def polynomial(terms, x):
+    value = terms[-1] * SCALE
+    for term in terms[-2::-1]:
+        value = value * x + term * SCALE
+    return value
+
+
+def scaled_turn(turn):
+    square = turn * turn
+    return polynomial(COS, square), turn * polynomial(SIN, square)
+
+
 def sign_matrix(count):
     both = lax.broadcasted_iota(jnp.int32, (count, count), 0) & lax.broadcasted_iota(jnp.int32, (count, count), 1)
     for shift in (4, 2, 1):
@@ -67,7 +86,7 @@
 def kernel(
     wave_ref, level_ref, angle_hbm, out_ref,
     wave, level, angle_ref, cosine, sine, local, local_in, send, recv, level_mid, level_in, mix, mix_in, back, back_in,
-    in_sem, pair_send, pair_recv, mid_send, mid_recv, level_send, level_recv, there_send, there_recv, back_send, back_recv, ready,
+    in_sem, pair_send, pair_recv, mid_send, mid_recv, level_send, level_recv, there_send, there_recv, back_send, back_recv, ready, beside,
 ):
     z, w, core = place()
     me = z * 16 + w
@@ -90,38 +109,47 @@
     angle_copy.start()
     wave_copy.start()
 
-    @pl.loop(1, 8)
-    def _(d):
-        signal(barrier, device((z + d) % 8, w, core))
-
-    @pl.loop(1, 16)
-    def _(d):
-        signal(barrier, device(z, plane_step(w, d), core))
-
-    signal(barrier, partner)
+    x, y = w % 2 * 2 + w // 8, w // 2 % 4
+    y_both = [device(z, plane(x, (y + d) % 4), core) for d in (1, 3)]
+    x_both = [device(z, plane((x + d) % 4, y), core) for d in (1, 3)]
+    for to in [device((z + d) % 8, w, core) for d in (4, 3, 5, 2, 6, 1, 7)] + y_both + x_both + [partner]:
+        signal(barrier, to)
 
     signs = sign_matrix(128)
-    level_copy.wait()
-
-    pl.semaphore_wait(barrier, 23)
-    for d in (4, 3, 5, 2, 6, 1, 7):
+
+    def send_levels(d):
         there = (z + d) % 8
         send_to(level.at[there], level_mid.at[z], mid_send, mid_recv.at[d - 1], device(there, w, core)).start()
+
+    def first_turns(start, stop):
+        @pl.loop(start, stop)
+        def _(b):
+            c, s = scaled_turn(angle_ref[0:1] * level[b])
+            re, im = wave[0, b], wave[1, b]
+            for part, value in enumerate((re * c + im * s, im * c - re * s)):
+                local[part, b] = turn_rows(turn_lanes(value, signs), signs)
+
+    pl.semaphore_wait(barrier, 12)
+    level_copy.wait()
+    for d in (4, 3, 5, 2, 6, 1, 7):
+        send_levels(d)
+    for to in y_both:
+        signal(beside.at[0], to)
+    angle_copy.wait()
+    wave_copy.wait()
+    for step in range(2):
+        first_turns(step * 2, step * 2 + 2)
+        pl.semaphore_wait(beside.at[step], 2)
+        for to in x_both:
+            signal(beside.at[step + 1], to)
+    first_turns(4, 6)
+    pl.semaphore_wait(beside.at[2], 2)
 
     @pl.loop(1, 16)
     def _(d):
         signal(ready, device(z, plane_step(w, d), core))
 
-    angle_copy.wait()
-    wave_copy.wait()
-
-    @pl.loop(0, 8)
-    def _(b):
-        turn = angle_ref[0:1] * level[b]
-        c, s = jnp.cos(turn) * SCALE, jnp.sin(turn) * SCALE
-        re, im = wave[0, b], wave[1, b]
-        for part, x in enumerate((re * c + im * s, im * c - re * s)):
-            local[part, b] = turn_rows(turn_lanes(x, signs), signs)
+    first_turns(6, 8)
 
     level_mid[z] = level[z]
 
@@ -153,11 +181,11 @@
                 send[0, b * 16 + t] = jnp.where(lower, re, pltpu.roll(im, 4, 0))
                 send[1, b * 16 + t] = jnp.where(lower, pltpu.roll(re, 4, 0), im)
 
-    def spread(src, dst, send_sem, recv_sem):
-        for d in (4, 3, 5, 2, 6, 1, 7, 0):
-
-            @pl.loop(0 if d else 1, 16)
-            def _(e):
+    def spread(src, dst, send_sem, recv_sem, steps=FAR_FIRST):
+        for e in steps:
+
+            @pl.loop(0 if e else 1, 8)
+            def _(d):
                 pz, pw = (z + d) % 8, plane_step(w, e)
                 send_to(src.at[pz * 16 + pw], dst.at[me], send_sem, recv_sem, device(pz, pw, core)).start()
 
@@ -171,7 +199,7 @@
         return back.at[k], back_in.at[k], back_send.at[k], back_recv.at[k]
 
     pl.semaphore_wait(ready, 15)
-    spread(*there(0))
+    spread(*there(0), steps=FAR_FIRST[:10])
     recv[0, me] = send[0, me]
 
     for d in (1, 7, 2, 6, 3, 5, 4):
@@ -188,6 +216,7 @@
         ).start()
 
     level_in[:, w] = level_mid[:, pl.ds(w * 8, 8)]
+    spread(*there(0), steps=FAR_FIRST[10:])
     spread(*there(1))
     recv[1, me] = send[1, me]
     level_part = level_in.at[:, pl.ds(0, 15)]
@@ -196,9 +225,8 @@
 
     @pl.loop(0, 8)
     def _(i):
-        turn = angle_ref[1:2] * level_in[i].reshape(128, 128)
-        cosine[i] = (jnp.cos(turn) * SCALE).reshape(16, 8, 128)
-        sine[i] = (jnp.sin(turn) * SCALE).reshape(16, 8, 128)
+        c, s = scaled_turn(angle_ref[1:2] * level_in[i].reshape(128, 128))
+        cosine[i], sine[i] = c.reshape(16, 8, 128), s.reshape(16, 8, 128)
 
     sublane = lax.broadcasted_iota(jnp.int32, (8, 128), 0)
 
@@ -295,7 +323,7 @@
     state, tiles = pltpu.VMEM((2, 8, 128, 128), f32), pltpu.VMEM((2, CHIPS, 8, 128), f32)
     table = pltpu.VMEM((8, 16, 8, 128), f32)
     blocks = pltpu.VMEM((8, 128, 128), f32)
-    dma = pltpu.SemaphoreType.DMA
+    dma, regular = pltpu.SemaphoreType.DMA, pltpu.SemaphoreType.REGULAR
     anywhere, on_chip = pl.BlockSpec(memory_space=pl.ANY), pl.BlockSpec(memory_space=pltpu.VMEM)
     off_chip = pl.BlockSpec(memory_space=pltpu.HBM)
     args = [pltpu.with_memory_space_constraint(x, pltpu.HBM) for x in (wave_parts, level_table, phase_angles)]
@@ -306,7 +334,7 @@
         out_specs=on_chip,
         scratch_shapes=[
             state, blocks, pltpu.VMEM((2, 128), f32), table, table, state, state, tiles, tiles, blocks, table, tiles, tiles, tiles, tiles,
-            dma((3,)), dma((6,)), dma((6,)), dma, dma((7,)), dma, dma, dma((2,)), dma((2,)), dma((2,)), dma((2,)), pltpu.SemaphoreType.REGULAR,
+            dma((3,)), dma((6,)), dma((6,)), dma, dma((7,)), dma, dma, dma((2,)), dma((2,)), dma((2,)), dma((2,)), regular, regular((3,)),
         ],
         compiler_params=pltpu.CompilerParams(collective_id=0, has_side_effects=True, vmem_limit_bytes=32 * 2**20),
     )(*args)

time: 73.7 us -> 69.7 us (0.946)
  Pallas kernels: 73.6 us -> 69.6 us
    pallas_call x1, Pallas kernels: 72.6 us -> 68.5 us  [body(): pl.pallas_call(kernel, out_shape=pltpu.VMEM((2, CHIPS, 8, 128), f32), in_...]
where the time goes in v3:
time: 69.7 us; the launch traced here: 69.6 us
  Pallas kernels  69.6 us (100%)
    pallas_call x1, Pallas kernels, body(): pl.pallas_call(kernel, out_shape=pltpu.VMEM((2, CHIPS, 8, 128), f32), in_...  68.5 us

profile of v3, /device:TPU:1, one launch (start us, length us, event | category | flops | bytes accessed | tf_op | source)
XLA Modules:
  0.0 69.6 jit_solution(1212510048537646314)
XLA Ops:
  0.0 68.5 %shard_map.37.tiles_ref = f32[2,128,8,128]{3,2,1,0:T(8,128)S(1)} custom-call(f32[2,8,128,128]{3,2,1,0:T(8,128)} %wave_ref.1, f32[8,128,128]{2,1,0:T(8,128)} %level_ref.1, f32[2,128]{1,0:T(2,128)} %angle_hbm.1), custom_call_target="tpu_custom_call" | custom-call | tf_op jit(solution)/shard_map/pallas_call | solution.py:330
  68.5 1.1 %shard_map.38 = f32[2,8,128,128]{3,2,1,0:T(8,128)} custom-call(f32[2,128,8,128]{3,2,1,0:T(8,128)S(1)} %shard_map.37.tiles_ref), custom_call_target="tpu_custom_call" | custom-call | tf_op jit(solution)/shard_map/pallas_call | solution.py:341

commit v4 on v3

--- a/solution.py
+++ b/solution.py
@@ -86,7 +86,7 @@
 def kernel(
     wave_ref, level_ref, angle_hbm, out_ref,
     wave, level, angle_ref, cosine, sine, local, local_in, send, recv, level_mid, level_in, mix, mix_in, back, back_in,
-    in_sem, pair_send, pair_recv, mid_send, mid_recv, level_send, level_recv, there_send, there_recv, back_send, back_recv, ready, beside,
+    in_sem, pair_send, pair_recv, mid_send, mid_recv, level_send, level_recv, there_send, there_recv, back_send, back_recv, ready, beside, far,
 ):
     z, w, core = place()
     me = z * 16 + w
@@ -112,7 +112,7 @@
     x, y = w % 2 * 2 + w // 8, w // 2 % 4
     y_both = [device(z, plane(x, (y + d) % 4), core) for d in (1, 3)]
     x_both = [device(z, plane((x + d) % 4, y), core) for d in (1, 3)]
-    for to in [device((z + d) % 8, w, core) for d in (4, 3, 5, 2, 6, 1, 7)] + y_both + x_both + [partner]:
+    for to in [device((z + d) % 8, w, core) for d in (2, 6, 1, 7)] + y_both + x_both + [partner]:
         signal(barrier, to)
 
     signs = sign_matrix(128)
@@ -129,20 +129,25 @@
             for part, value in enumerate((re * c + im * s, im * c - re * s)):
                 local[part, b] = turn_rows(turn_lanes(value, signs), signs)
 
-    pl.semaphore_wait(barrier, 12)
+    pl.semaphore_wait(barrier, 9)
+    for i, d in enumerate((7, 1, 6)):
+        signal(far.at[i], device((z + d) % 8, w, core))
     level_copy.wait()
-    for d in (4, 3, 5, 2, 6, 1, 7):
+    for d in (1, 7, 2, 6):
         send_levels(d)
     for to in y_both:
         signal(beside.at[0], to)
     angle_copy.wait()
     wave_copy.wait()
+    first_turns(0, 2)
+    for i, d in enumerate((3, 5, 4)):
+        pl.semaphore_wait(far.at[i], 1)
+        send_levels(d)
     for step in range(2):
-        first_turns(step * 2, step * 2 + 2)
         pl.semaphore_wait(beside.at[step], 2)
         for to in x_both:
             signal(beside.at[step + 1], to)
-    first_turns(4, 6)
+        first_turns(2 + step * 2, 4 + step * 2)
     pl.semaphore_wait(beside.at[2], 2)
 
     @pl.loop(1, 16)
@@ -150,7 +155,6 @@
         signal(ready, device(z, plane_step(w, d), core))
 
     first_turns(6, 8)
-
     level_mid[z] = level[z]
 
     def swap(q):
@@ -199,7 +203,7 @@
         return back.at[k], back_in.at[k], back_send.at[k], back_recv.at[k]
 
     pl.semaphore_wait(ready, 15)
-    spread(*there(0), steps=FAR_FIRST[:10])
+    spread(*there(0), steps=FAR_FIRST[:13])
     recv[0, me] = send[0, me]
 
     for d in (1, 7, 2, 6, 3, 5, 4):
@@ -216,7 +220,7 @@
         ).start()
 
     level_in[:, w] = level_mid[:, pl.ds(w * 8, 8)]
-    spread(*there(0), steps=FAR_FIRST[10:])
+    spread(*there(0), steps=FAR_FIRST[13:])
     spread(*there(1))
     recv[1, me] = send[1, me]
     level_part = level_in.at[:, pl.ds(0, 15)]
@@ -293,6 +297,13 @@
             for j, x in enumerate(fwht([back_in[k, i * 16 + j] for j in range(16)])):
                 out_ref[k, i * 16 + j] = x
 
+        if k == 0:
+
+            @pl.loop(0, 16)
+            def _(j):
+                for i, x in enumerate(fwht([out_ref[k, i * 16 + j] for i in range(8)])):
+                    out_ref[k, i * 16 + j] = x
+
     for k in range(2):
         gathered(*again(k)).wait_send()
 
@@ -300,18 +311,19 @@
 def finish(tiles_ref, out_ref, final, out_sem):
     lower = lax.broadcasted_iota(jnp.int32, (8, 128), 0) < 4
     copies = []
-    for q in range(4):
-
-        @pl.loop(q * 4, q * 4 + 4)
+    for q in range(8):
+
+        @pl.loop(q * 2, q * 2 + 2)
         def _(j):
-            first, second = (fwht([tiles_ref[k, i * 16 + j] for i in range(8)]) for k in range(2))
+            first, second = ([tiles_ref[k, i * 16 + j] for i in range(8)] for k in range(2))
+            second = fwht(second)
             rows = pl.ds(j * 8, 8)
             for i in range(8):
                 u, v = first[i] + second[i], first[i] - second[i]
                 final[0, i, rows] = jnp.where(lower, u, pltpu.roll(v, 4, 0))
                 final[1, i, rows] = jnp.where(lower, pltpu.roll(u, 4, 0), v)
 
-        rows = pl.ds(q * 32, 32)
+        rows = pl.ds(q * 16, 16)
         copies.append(pltpu.make_async_copy(final.at[:, :, rows], out_ref.at[:, :, rows], out_sem.at[q]))
         copies[-1].start()
     for copy in copies:
@@ -334,7 +346,7 @@
         out_specs=on_chip,
         scratch_shapes=[
             state, blocks, pltpu.VMEM((2, 128), f32), table, table, state, state, tiles, tiles, blocks, table, tiles, tiles, tiles, tiles,
-            dma((3,)), dma((6,)), dma((6,)), dma, dma((7,)), dma, dma, dma((2,)), dma((2,)), dma((2,)), dma((2,)), regular, regular((3,)),
+            dma((3,)), dma((6,)), dma((6,)), dma, dma((7,)), dma, dma, dma((2,)), dma((2,)), dma((2,)), dma((2,)), regular, regular((3,)), regular((3,)),
         ],
         compiler_params=pltpu.CompilerParams(collective_id=0, has_side_effects=True, vmem_limit_bytes=32 * 2**20),
     )(*args)
@@ -343,7 +355,7 @@
         out_shape=jax.ShapeDtypeStruct(wave_parts.shape, f32),
         in_specs=[on_chip],
         out_specs=anywhere,
-        scratch_shapes=[state, dma((4,))],
+        scratch_shapes=[state, dma((8,))],
         compiler_params=pltpu.CompilerParams(vmem_limit_bytes=16 * 2**20),
     )(mixed)
 

time: 69.7 us -> 69 us (0.990)
  Pallas kernels: 69.6 us -> 68.8 us
    pallas_call x1, Pallas kernels: 68.5 us -> 67.8 us  [body(): pl.pallas_call(kernel, out_shape=pltpu.VMEM((2, CHIPS, 8, 128), f32), in_...]
where the time goes in v4:
time: 69 us; the launch traced here: 68.8 us
  Pallas kernels  68.8 us (100%)
    pallas_call x1, Pallas kernels, body(): pl.pallas_call(kernel, out_shape=pltpu.VMEM((2, CHIPS, 8, 128), f32), in_...  67.8 us

profile of v4, /device:TPU:1, one launch (start us, length us, event | category | flops | bytes accessed | tf_op | source)
XLA Modules:
  0.0 68.8 jit_solution(2444792756595010084)
XLA Ops:
  0.0 67.8 %shard_map.37.tiles_ref = f32[2,128,8,128]{3,2,1,0:T(8,128)S(1)} custom-call(f32[2,8,128,128]{3,2,1,0:T(8,128)} %wave_ref.1, f32[8,128,128]{2,1,0:T(8,128)} %level_ref.1, f32[2,128]{1,0:T(2,128)} %angle_hbm.1), custom_call_target="tpu_custom_call" | custom-call | tf_op jit(solution)/shard_map/pallas_call | solution.py:342
  67.8 1.1 %shard_map.38 = f32[2,8,128,128]{3,2,1,0:T(8,128)} custom-call(f32[2,128,8,128]{3,2,1,0:T(8,128)S(1)} %shard_map.37.tiles_ref), custom_call_target="tpu_custom_call" | custom-call | tf_op jit(solution)/shard_map/pallas_call | solution.py:353

commit v5 on v4

--- a/solution.py
+++ b/solution.py
@@ -107,7 +107,6 @@
     level_copy.start()
     angle_copy = pltpu.make_async_copy(angle_hbm, angle_ref, in_sem.at[2])
     angle_copy.start()
-    wave_copy.start()
 
     x, y = w % 2 * 2 + w // 8, w // 2 % 4
     y_both = [device(z, plane(x, (y + d) % 4), core) for d in (1, 3)]
@@ -115,6 +114,7 @@
     for to in [device((z + d) % 8, w, core) for d in (2, 6, 1, 7)] + y_both + x_both + [partner]:
         signal(barrier, to)
 
+    wave_copy.start()
     signs = sign_matrix(128)
 
     def send_levels(d):

time: 69 us -> 69 us (level)
  no operation moved by 1% of the time
where the time goes in v5:
time: 69 us; the launch traced here: 68.8 us
  Pallas kernels  68.8 us (100%)
    pallas_call x1, Pallas kernels, body(): pl.pallas_call(kernel, out_shape=pltpu.VMEM((2, CHIPS, 8, 128), f32), in_...  67.7 us

profile of v5, /device:TPU:1, one launch (start us, length us, event | category | flops | bytes accessed | tf_op | source)
XLA Modules:
  0.0 68.8 jit_solution(15983532273346101610)
XLA Ops:
  0.0 67.7 %shard_map.37.tiles_ref = f32[2,128,8,128]{3,2,1,0:T(8,128)S(1)} custom-call(f32[2,8,128,128]{3,2,1,0:T(8,128)} %wave_ref.1, f32[8,128,128]{2,1,0:T(8,128)} %level_ref.1, f32[2,128]{1,0:T(2,128)} %angle_hbm.1), custom_call_target="tpu_custom_call" | custom-call | tf_op jit(solution)/shard_map/pallas_call | solution.py:342
  67.8 1.1 %shard_map.38 = f32[2,8,128,128]{3,2,1,0:T(8,128)} custom-call(f32[2,128,8,128]{3,2,1,0:T(8,128)S(1)} %shard_map.37.tiles_ref), custom_call_target="tpu_custom_call" | custom-call | tf_op jit(solution)/shard_map/pallas_call | solution.py:353

commit v6 on v5

--- a/solution.py
+++ b/solution.py
@@ -190,7 +190,7 @@
 
             @pl.loop(0 if e else 1, 8)
             def _(d):
-                pz, pw = (z + d) % 8, plane_step(w, e)
+                pz, pw = (z + d + (core * 4 if e else 0)) % 8, plane_step(w, e)
                 send_to(src.at[pz * 16 + pw], dst.at[me], send_sem, recv_sem, device(pz, pw, core)).start()
 
     def gathered(src, dst, send_sem, recv_sem):

time: 69 us -> 69 us (level)
  no operation moved by 1% of the time
where the time goes in v6:
time: 69 us; the launch traced here: 68.9 us
  Pallas kernels  68.9 us (100%)
    pallas_call x1, Pallas kernels, body(): pl.pallas_call(kernel, out_shape=pltpu.VMEM((2, CHIPS, 8, 128), f32), in_...  67.8 us

profile of v6, /device:TPU:1, one launch (start us, length us, event | category | flops | bytes accessed | tf_op | source)
XLA Modules:
  0.0 68.9 jit_solution(13009839796039261697)
XLA Ops:
  0.0 67.8 %shard_map.37.tiles_ref = f32[2,128,8,128]{3,2,1,0:T(8,128)S(1)} custom-call(f32[2,8,128,128]{3,2,1,0:T(8,128)} %wave_ref.1, f32[8,128,128]{2,1,0:T(8,128)} %level_ref.1, f32[2,128]{1,0:T(2,128)} %angle_hbm.1), custom_call_target="tpu_custom_call" | custom-call | tf_op jit(solution)/shard_map/pallas_call | solution.py:342
  67.8 1.1 %shard_map.38 = f32[2,8,128,128]{3,2,1,0:T(8,128)} custom-call(f32[2,128,8,128]{3,2,1,0:T(8,128)S(1)} %shard_map.37.tiles_ref), custom_call_target="tpu_custom_call" | custom-call | tf_op jit(solution)/shard_map/pallas_call | solution.py:353
